TPU v7x, 32 devices: a whole 2x2x4 slice. The times are simulated.
32 devices in a mesh: rows: 16 (over z, y, x), cols: 2 (over core).
Axes of the slice: x: 2, y: 2, z: 4, core: 2. Of those that a mesh axis runs over, the one named last changes fastest.
Arguments:
- eigvecs: float32 [4096, 2048], P('rows', 'cols'), may hold values from -6 to 6
- reflectors: float32 [32, 4096], P('cols', 'rows'), may hold values from -17 to 17
- starts: int32 [32], replicated, may hold values from 0 to 63
Outputs:
- rotated: float32 [4096, 2048], P('rows', 'cols')
Inputs may be any that keep to these rules, and one draw needn't show every extreme that they name: Sweep j's windows begin at rows starts[j] + k * 64.
All inputs are finite; a program needn't handle non-finite values.
Results may differ from a plain program's by a relative error of at most 0.00011.
Values sent between devices are 32-bit elements; how exact they have to be, the bound alone decides.
A program may use at most 64 MiB of HBM per device.

v0:
```python
import jax
import jax.numpy as jnp
from jax import lax
from jax.sharding import PartitionSpec as P

BAND = 64
SWEEPS = 32


def column_sweep(turned, reflector, offset):
    width = turned.shape[0]
    total_rows = turned.shape[1]
    blocks = total_rows // BAND
    rolled = jnp.roll(turned, -offset, axis=1).reshape(width, blocks, BAND)
    rolled_v = jnp.roll(reflector, -offset).reshape(blocks, BAND)
    squares = jnp.sum(rolled_v * rolled_v, axis=1)
    window = jnp.arange(blocks, dtype=jnp.int32)
    usable = (window + 1) * BAND + offset <= total_rows
    scaled = jnp.where(usable, 2.0 / jnp.where(usable, squares, 1.0), 0.0)
    products = jnp.sum(rolled * rolled_v[None, :, :], axis=2)
    rolled = rolled - (products * scaled[None, :])[:, :, None] * rolled_v[None, :, :]
    return jnp.roll(rolled.reshape(width, total_rows), offset, axis=1)


def per_device(eigvecs, reflectors, starts):
    every_sweep = lax.all_gather(reflectors, "cols", axis=0, tiled=True)
    turned = lax.all_to_all(eigvecs, "rows", split_axis=1, concat_axis=0, tiled=True)
    whole_v = lax.all_gather(every_sweep, "rows", axis=1, tiled=True)
    crossed = turned.T

    def advance(sweep_idx, state):
        return column_sweep(state, whole_v[sweep_idx], starts[sweep_idx])

    crossed = lax.fori_loop(0, SWEEPS, advance, crossed)
    return lax.all_to_all(crossed.T, "rows", split_axis=0, concat_axis=1, tiled=True)


def solution(mesh):
    in_specs = (P("rows", "cols"), P("cols", "rows"), P())
    out_specs = P("rows", "cols")
    return jax.shard_map(
        per_device, mesh=mesh, in_specs=in_specs, out_specs=out_specs, check_vma=False
    )
```

profile of v0, /device:TPU:0, one launch (start us, length us, event | category | flops | bytes accessed | tf_op | source)
XLA Modules:
  0.0 527.9 jit_solution(18121734052208252811)
XLA Ops:
  0.0 2.5 copy.12
  2.5 8.5 %all-to-all-start = ((f32[256,16,64]{0,2,1:T(8,128)}), f32[256,16,64]{0,2,1:T(8,128)S(1)}, u32[]{:S(2)}, u32[]{:S(2)}) async-start(f32[256,16,64]{0,2,1:T(8,128)} %bitcast.2), calls=%async_computation | async-start | bytes 2097152 | tf_op jit(solution)/shard_map/all_to_all | solution.py:27
  12.9 55.0 %all_gather.7 = f32[32,4096]{1,0:T(8,128)} all-gather(f32[32,256]{1,0:T(8,128)S(1)} %all_gather.6), channel_id=1, replica_groups=mesh['rows'=16,'cols'=2] {'rows'}, dimensions={1}, use_global_device_ids=true | all-gather | bytes 557056 | tf_op jit(solution)/shard_map/all_gather | solution.py:28
  68.0 435.8 %while.15 = (s32[]{:T(128)}, f32[64,4096]{1,0:T(8,128)S(1)}, s32[32]{0:T(128)S(1)}, f32[32,4096]{1,0:T(8,128)}, s32[]{:T(128)}, /*index=5*/s32[]{:T(128)}, s32[]{:T(128)}, s32[]{:T(128)}, s32[]{:T(128)}) while((s32[]{:T(128)}, f32[64,4096]{1,0:T(8,128)S(1)}, s32[32]{0:T(128)S(1)}, f32[32,4096]{1,0:T(8,128)}, s32[]{:T(128)}, ...), condition=%wide.region_3.5_spmd, body=%wide.region_0.4_spmd.sunk | while | flops 1847711 | bytes 13845943 | solution.py:34
  72.5 2.0 reshape.75
  86.1 2.0 reshape.75
  99.7 2.0 reshape.75
  113.3 2.0 reshape.75
  126.9 2.0 reshape.75
  140.6 2.0 reshape.75
  154.2 2.0 reshape.75
  167.8 2.0 reshape.75
  181.4 2.0 reshape.75
  195.0 2.0 reshape.75
  208.7 2.0 reshape.75
  222.3 2.0 reshape.75
  235.9 2.0 reshape.75
  249.5 2.0 reshape.75
  263.1 2.0 reshape.75
  276.8 2.0 reshape.75
  290.4 2.0 reshape.75
  304.0 2.0 reshape.75
  317.6 2.0 reshape.75
  331.2 2.0 reshape.75
  344.9 2.0 reshape.75
  358.5 2.0 reshape.75
  372.1 2.0 reshape.75
  385.7 2.0 reshape.75
  399.3 2.0 reshape.75
  453.8 2.0 reshape.75
  494.7 2.0 reshape.75
  503.9 22.7 %all_to_all.38 = f32[16,256,64]{1,2,0:T(8,128)S(1)} all-to-all(f32[16,256,64]{1,2,0:T(8,128)S(1)} %bitcast.23), channel_id=1, replica_groups=mesh['rows'=16,'cols'=2] {'rows'}, dimensions={0} | all-to-all | bytes 2097152 | tf_op jit(solution)/shard_map/all_to_all | solution.py:35
  (430 shorter events, 309.5 us)
Async XLA Ops:
  0.0 11.0 %copy-start = (f32[16,256]{1,0:T(8,128)S(1)}, f32[16,256]{1,0:T(8,128)}, u32[]{:S(2)}) copy-start(f32[16,256]{1,0:T(8,128)} %param.8) | copy-start | bytes 49156
  2.5 65.4 %copy-start.1 = (s32[32]{0:T(128)S(1)}, s32[32]{0:T(128)}, u32[]{:S(2)}) copy-start(s32[32]{0:T(128)} %param.9) | copy-start | bytes 388
  2.5 65.3 %all-to-all-start = ((f32[256,16,64]{0,2,1:T(8,128)}), f32[256,16,64]{0,2,1:T(8,128)S(1)}, u32[]{:S(2)}, u32[]{:S(2)}) async-start(f32[256,16,64]{0,2,1:T(8,128)} %bitcast.2), calls=%async_computation | async-start | bytes 2097152 | tf_op jit(solution)/shard_map/all_to_all | solution.py:27
where the time goes:
time: 532 us; the launch traced here: 528 us
  local copies, waits for them, and re-layouts  190 us (36%)
  other arithmetic  174 us (33%)
  blocking collectives  79.5 us (15%)
  loops' own time  75.8 us (14%)
  starting transfers between devices  8.47 us (2%)
    another operation x1, loops' own time, per_device(): crossed = lax.fori_loop(0, SWEEPS, advance, crossed)  75.8 us
    mul x64, local copies, waits for them, and re-layouts, column_sweep(): (products * scaled[None, :])[:, :, None] * rolled_v[None, :, :]  71.3 us
    reshape x32, local copies, waits for them, and re-layouts, column_sweep(): rolled = jnp.roll(turned, -offset, axis=1).reshape(width, blocks, BAND)  63.9 us
    sub x32, other arithmetic, column_sweep(): rolled - (products * scaled[None, :])[:, :, None] * rolled_v[None, :, :]  58.7 us
    all_gather x1, blocking collectives, per_device(): whole_v = lax.all_gather(every_sweep, 'rows', axis=1, tiled=True)  55 us
    concatenate x32, other arithmetic, column_sweep(): rolled = jnp.roll(turned, -offset, axis=1).reshape(width, blocks, BAND)  50.8 us
    dynamic_slice x64, local copies, waits for them, and re-layouts, advance(): return column_sweep(state, whole_v[sweep_idx], starts[sweep_idx])  48.1 us
    all_to_all x1, blocking collectives, per_device(): lax.all_to_all(crossed.T, 'rows', split_axis=0, concat_axis=1, tiled=True)  22.7 us
  transfers between devices with their start and end apart: 1, of which 0 were waited for; matrix products, arithmetic and copies ran while one was open for 0% of the time, Pallas kernels for 0%

commit v1 on v0

--- a/solution.py
+++ b/solution.py
@@ -25,7 +25,7 @@
 def per_device(eigvecs, reflectors, starts):
     every_sweep = lax.all_gather(reflectors, "cols", axis=0, tiled=True)
     turned = lax.all_to_all(eigvecs, "rows", split_axis=1, concat_axis=0, tiled=True)
-    whole_v = lax.all_gather(every_sweep, "rows", axis=1, tiled=True)
+    whole_v = jnp.concatenate(lax.all_gather(every_sweep, "rows"), axis=1)
     crossed = turned.T
 
     def advance(sweep_idx, state):

time: 532 us -> 531 us (level)
  no operation moved by 1% of the time
where the time goes in v1:
time: 531 us; the launch traced here: 527 us
  local copies, waits for them, and re-layouts  191 us (36%)
  other arithmetic  174 us (33%)
  blocking collectives  77.4 us (15%)
  loops' own time  75.8 us (14%)
  starting transfers between devices  8.34 us (2%)
    another operation x1, loops' own time, per_device(): crossed = lax.fori_loop(0, SWEEPS, advance, crossed)  75.8 us
    mul x64, local copies, waits for them, and re-layouts, column_sweep(): (products * scaled[None, :])[:, :, None] * rolled_v[None, :, :]  71.3 us
    reshape x32, local copies, waits for them, and re-layouts, column_sweep(): rolled = jnp.roll(turned, -offset, axis=1).reshape(width, blocks, BAND)  63.9 us
    sub x32, other arithmetic, column_sweep(): rolled - (products * scaled[None, :])[:, :, None] * rolled_v[None, :, :]  58.7 us
    all_gather x1, blocking collectives, per_device(): whole_v = jnp.concatenate(lax.all_gather(every_sweep, 'rows'), axis=1)  52.7 us
    concatenate x32, other arithmetic, column_sweep(): rolled = jnp.roll(turned, -offset, axis=1).reshape(width, blocks, BAND)  50.8 us
    dynamic_slice x64, local copies, waits for them, and re-layouts, advance(): return column_sweep(state, whole_v[sweep_idx], starts[sweep_idx])  48.1 us
    all_to_all x1, blocking collectives, per_device(): lax.all_to_all(crossed.T, 'rows', split_axis=0, concat_axis=1, tiled=True)  22.9 us
  transfers between devices with their start and end apart: 1, of which 0 were waited for; matrix products, arithmetic and copies ran while one was open for 0% of the time, Pallas kernels for 0%

profile of v1, /device:TPU:0, one launch (start us, length us, event | category | flops | bytes accessed | tf_op | source)
XLA Modules:
  0.0 526.5 jit_solution(9435078000530873760)
XLA Ops:
  0.0 2.5 copy.15
  2.5 8.3 %all-to-all-start = ((f32[256,16,64]{0,2,1:T(8,128)}), f32[256,16,64]{0,2,1:T(8,128)S(1)}, u32[]{:S(2)}, u32[]{:S(2)}) async-start(f32[256,16,64]{0,2,1:T(8,128)} %bitcast.2), calls=%async_computation | async-start | bytes 2097152 | tf_op jit(solution)/shard_map/all_to_all | solution.py:27
  12.7 52.7 %all-gather = f32[512,256]{1,0:T(8,128)S(1)} all-gather(f32[32,256]{1,0:T(8,128)S(1)} %all_gather.9), channel_id=2, replica_groups=mesh['rows'=16,'cols'=2] {'rows'}, dimensions={0}, use_global_device_ids=true | all-gather | bytes 557056 | tf_op jit(solution)/shard_map/all_gather | solution.py:28
  66.4 435.8 %while.15 = (s32[]{:T(128)}, f32[64,4096]{1,0:T(8,128)S(1)}, s32[32]{0:T(128)S(1)}, f32[32,4096]{1,0:T(8,128)}, s32[]{:T(128)}, /*index=5*/s32[]{:T(128)}, s32[]{:T(128)}, s32[]{:T(128)}, s32[]{:T(128)}) while((s32[]{:T(128)}, f32[64,4096]{1,0:T(8,128)S(1)}, s32[32]{0:T(128)S(1)}, f32[32,4096]{1,0:T(8,128)}, s32[]{:T(128)}, ...), condition=%wide.region_3.5_spmd, body=%wide.region_0.4_spmd.sunk | while | flops 1847711 | bytes 13845943 | solution.py:34
  70.9 2.0 reshape.84
  84.5 2.0 reshape.84
  98.1 2.0 reshape.84
  111.7 2.0 reshape.84
  125.3 2.0 reshape.84
  138.9 2.0 reshape.84
  152.6 2.0 reshape.84
  166.2 2.0 reshape.84
  179.8 2.0 reshape.84
  193.4 2.0 reshape.84
  207.0 2.0 reshape.84
  220.7 2.0 reshape.84
  234.3 2.0 reshape.84
  247.9 2.0 reshape.84
  261.5 2.0 reshape.84
  275.1 2.0 reshape.84
  288.8 2.0 reshape.84
  302.4 2.0 reshape.84
  316.0 2.0 reshape.84
  329.6 2.0 reshape.84
  343.2 2.0 reshape.84
  356.9 2.0 reshape.84
  370.5 2.0 reshape.84
  384.1 2.0 reshape.84
  397.7 2.0 reshape.84
  411.3 2.0 reshape.84
  425.0 2.0 reshape.84
  502.3 22.9 %all_to_all.38 = f32[16,256,64]{1,2,0:T(8,128)S(1)} all-to-all(f32[16,256,64]{1,2,0:T(8,128)S(1)} %bitcast.29), channel_id=1, replica_groups=mesh['rows'=16,'cols'=2] {'rows'}, dimensions={0} | all-to-all | bytes 2097152 | tf_op jit(solution)/shard_map/all_to_all | solution.py:35
  (431 shorter events, 310.3 us)
Async XLA Ops:
  0.0 10.9 %copy-start = (f32[16,256]{1,0:T(8,128)S(1)}, f32[16,256]{1,0:T(8,128)}, u32[]{:S(2)}) copy-start(f32[16,256]{1,0:T(8,128)} %param.8) | copy-start | bytes 49156
  2.5 63.7 %all-to-all-start = ((f32[256,16,64]{0,2,1:T(8,128)}), f32[256,16,64]{0,2,1:T(8,128)S(1)}, u32[]{:S(2)}, u32[]{:S(2)}) async-start(f32[256,16,64]{0,2,1:T(8,128)} %bitcast.2), calls=%async_computation | async-start | bytes 2097152 | tf_op jit(solution)/shard_map/all_to_all | solution.py:27
  10.9 55.5 %copy-start.1 = (s32[32]{0:T(128)S(1)}, s32[32]{0:T(128)}, u32[]{:S(2)}) copy-start(s32[32]{0:T(128)} %param.9) | copy-start | bytes 388
